TPU v7x, 32 devices: a whole 2x2x4 slice. The times are simulated.
32 devices in a mesh: gx: 2 (over core), gy: 4 (over y, x), gz: 4 (over z).
Axes of the slice: x: 2, y: 2, z: 4, core: 2. Of those that a mesh axis runs over, the one named last changes fastest.
Arguments:
- raw_weight: float32 [128, 27, 128], P(('gx', 'gy')), may hold values from -6 to 6
- inputs: bfloat16 [16, 64, 64, 128], P('gx', 'gy', 'gz'), may hold values from -6 to 6
- cotangent: bfloat16 [16, 64, 64, 128], P('gx', 'gy', 'gz'), may hold values from -0.099609375 to 0.099609375
Outputs:
- input_grad: bfloat16 [16, 64, 64, 128], P('gx', 'gy', 'gz')
- weight_grad: float32 [128, 27, 128], P(('gx', 'gy'))
All inputs are finite; a program needn't handle non-finite values.
Results may differ from a plain program's by a relative error of at most 0.0049.
Values may be sent and summed in bfloat16 or wider, within the bound.
A program may use at most 64 MiB of HBM per device.

v0:
```python
import jax
import jax.numpy as jnp
from jax import lax
from jax.sharding import PartitionSpec as P

var_eps = 1e-05
norm_eps = 1e-06
clip_norm = 600.0


def with_halo(cells, sides, width):
    for axis, dim in sides:
        count = lax.axis_size(axis)
        ends = count - 1
        head = lax.slice_in_dim(cells, 0, width, axis=dim)
        tail = lax.slice_in_dim(cells, cells.shape[dim] - width, cells.shape[dim], axis=dim)
        cells = jnp.concatenate(
            [
                lax.ppermute(tail, axis, [(i, (i + 1) % count) for i in range(ends)]),
                cells,
                lax.ppermute(head, axis, [((i + 1) % count, i) for i in range(ends)]),
            ],
            axis=dim,
        )
    return cells


def tap_view(padded, tap_a, tap_b, tap_c, extent):
    view = padded[
        2 - tap_a : 2 - tap_a + extent[0],
        2 - tap_b : 2 - tap_b + extent[1],
        2 - tap_c : 2 - tap_c + extent[2],
        :,
    ]
    return view.reshape(-1, view.shape[-1])


def input_rows(padded, extent, block_rows):
    row_count = block_rows.shape[0]
    total = jnp.zeros((extent[0] * extent[1] * extent[2], row_count), jnp.float32)
    for tap_a in range(3):
        for tap_b in range(3):
            for tap_c in range(3):
                tap_index = tap_a * 9 + tap_b * 3 + tap_c
                view = tap_view(padded, tap_a, tap_b, tap_c, extent)
                total = total + lax.dot_general(
                    view,
                    block_rows[:, tap_index, :],
                    (((1,), (1,)), ((), ())),
                    preferred_element_type=jnp.float32,
                )
    return total.astype(jnp.bfloat16).reshape(extent[0], extent[1], extent[2], row_count)


def filter_terms(padded, flat_in, extent):
    pieces = []
    for tap_a in range(3):
        for tap_b in range(3):
            for tap_c in range(3):
                view = tap_view(padded, tap_a, tap_b, tap_c, extent)
                pieces.append(
                    lax.dot_general(
                        flat_in, view, (((0,), (0,)), ((), ())), preferred_element_type=jnp.float32
                    )
                )
    return jnp.stack(pieces, axis=1)


def on_device(raw_weight, inputs, cotangent):
    extent = inputs.shape[:3]
    channels = inputs.shape[3]
    fan_count = channels * raw_weight.shape[1]
    padded = with_halo(cotangent, (("gx", 0), ("gy", 1), ("gz", 2)), 1)
    flat_in = inputs.reshape(-1, channels)
    sum_first, sum_second = lax.psum(
        (jnp.sum(raw_weight, axis=(0, 1)), jnp.sum(raw_weight * raw_weight, axis=(0, 1))),
        ("gx", "gy"),
    )
    mean_out = sum_first / fan_count
    var_out = sum_second / fan_count - mean_out * mean_out
    inv_std = lax.rsqrt(var_out + var_eps)
    std_float = (raw_weight - mean_out) * inv_std
    std_whole = lax.all_gather(std_float.astype(jnp.bfloat16), ("gx", "gy"), axis=0, tiled=True)
    input_grad = input_rows(padded, extent, std_whole)
    local_terms = filter_terms(padded, flat_in, extent)
    column_sum = lax.psum(local_terms, "gz")
    filter_grad = lax.psum_scatter(column_sum, ("gx", "gy"), scatter_dimension=0, tiled=True)
    local_grad = jnp.sum(filter_grad, axis=(0, 1))
    local_cross = jnp.sum(filter_grad * std_float, axis=(0, 1))
    local_square = jnp.sum(filter_grad * filter_grad, axis=(0, 1))
    sum_grad, sum_cross, sum_square = lax.psum(
        (local_grad, local_cross, local_square), ("gx", "gy")
    )
    mean_grad = sum_grad / fan_count
    mean_cross = sum_cross / fan_count
    raw_grad = inv_std * (filter_grad - mean_grad - std_float * mean_cross)
    per_output = sum_square - 2.0 * mean_grad * sum_grad - 2.0 * mean_cross * sum_cross
    per_output = (
        per_output
        + fan_count * mean_grad * mean_grad
        + fan_count * mean_cross * mean_cross * var_out / (var_out + var_eps)
    )
    square_sum = jnp.sum(inv_std * inv_std * per_output)
    scale = jnp.minimum(1.0, clip_norm * lax.rsqrt(square_sum + norm_eps))
    return (input_grad, raw_grad * scale)


def solution(mesh):
    in_specs = (P(("gx", "gy"), None, None), P("gx", "gy", "gz", None), P("gx", "gy", "gz", None))
    out_specs = (P("gx", "gy", "gz", None), P(("gx", "gy"), None, None))
    return jax.shard_map(
        on_device, mesh=mesh, in_specs=in_specs, out_specs=out_specs, check_vma=False
    )
```

profile of v0, /device:TPU:0, one launch (start us, length us, event | category | flops | bytes accessed | tf_op | source)
XLA Modules:
  0.0 215.6 jit_solution(4366381669883090917)
XLA Ops:
  8.2 2.4 %collective-permute-start = (bf16[1,16,16,128]{3,2,1,0:T(8,128)(2,1)S(1)}, bf16[1,16,16,128]{3,2,1,0:T(8,128)(2,1)S(1)}, u32[]{:S(2)}, u32[]{:S(2)}) collective-permute-start(bf16[1,16,16,128]{3,2,1,0:T(8,128)(2,1)S(1)} %get-tuple-element.51), channel_id=1, source_target_pairs={{0,16},{1,17},{2,18},{3,19},{4,20},{5,21},{6,22},{7,23},{8,24},{9,... | collective-permute-start | bytes 196616 | tf_op jit(solution)/shard_map/ppermute | solution.py:19
  10.6 1.3 collective-permute-start.1
  11.9 1.4 constant_dynamic-update-slice_fusion.5
  13.8 1.3 collective-permute-start.3
  15.1 4.8 %collective-permute-start.2 = (bf16[10,1,16,128]{3,2,1,0:T(8,128)(2,1)S(1)}, bf16[10,1,16,128]{3,2,1,0:T(8,128)(2,1)S(1)}, u32[]{:S(2)}, u32[]{:S(2)}) collective-permute-start(bf16[10,1,16,128]{3,2,1,0:T(8,128)(2,1)S(1)} %get-tuple-element.45), channel_id=1, source_target_pairs={{0,4},{4,8},{8,12},{1,5},{5,9},{9,13},{2,6},{6,10},{10,14},{3,7},{... | collective-permute-start | bytes 122888 | tf_op jit(solution)/shard_map/ppermute | solution.py:19
  20.3 1.3 collective-permute-done.2
  21.8 1.3 collective-permute-start.4
  23.1 4.6 %collective-permute-start.5 = (bf16[10,18,1,128]{3,2,1,0:T(2,128)(2,1)S(1)}, bf16[10,18,1,128]{3,2,1,0:T(2,128)(2,1)S(1)}, u32[]{:S(2)}, u32[]{:S(2)}) collective-permute-start(bf16[10,18,1,128]{3,2,1,0:T(2,128)(2,1)S(1)} %get-tuple-element.35), channel_id=1, source_target_pairs={{0,1},{1,2},{2,3},{4,5},{5,6},{6,7},{8,9},{9,10},{10,11},{12,13},{... | collective-permute-start | bytes 138248 | tf_op jit(solution)/shard_map/ppermute | solution.py:19
  28.3 1.5 collective-permute-done.5
  30.6 1.0 fusion.29
  31.6 1.0 fusion.10
  32.6 1.0 fusion.28
  33.5 1.0 fusion.27
  34.5 1.0 fusion.9
  35.5 1.0 fusion.26
  36.5 1.0 fusion.25
  37.4 1.0 fusion.8
  38.4 1.0 fusion.24
  39.4 1.0 fusion.23
  40.4 1.0 fusion.7
  42.3 1.0 fusion.21
  43.3 1.0 fusion.20
  44.3 1.0 fusion.19
  45.3 1.0 fusion.18
  46.3 1.0 fusion.6
  47.2 1.0 fusion.17
  48.2 1.0 fusion.16
  51.1 1.0 fusion.14
  52.1 1.0 fusion.4
  53.1 1.0 fusion.13
  54.1 1.0 fusion.12
  55.0 1.0 fusion.3
  56.0 1.0 fusion.11
  57.0 3.1 %copy.12 = f32[128,27,128]{2,1,0:T(8,128)} copy(f32[128,27,128]{0,2,1:T(8,128)} %fusion.11) | data formatting | bytes 3538944 | tf_op jit(solution)/shard_map/stack | solution.py:66
  60.2 1.0 multiply_reduce_fusion.2
  61.2 16.7 %all-reduce.1 = (f32[128]{0:T(128)S(1)}, f32[128]{0:T(128)S(1)}) all-reduce(f32[128]{0:T(128)S(1)} %get-tuple-element.8, f32[128]{0:T(128)S(1)} %get-tuple-element.7), channel_id=1, replica_groups=mesh['gx'=2,'gy'=4,'gz'=4] {'gx','gy'}, use_global_device_ids=true, to_apply=%region_1.0 | all-reduce | flops 256 | bytes 2048 | tf_op jit(solution)/shard_map/psum | solution.py:75
  77.9 1.9 slice.299
  79.8 1.9 slice.338
  81.7 1.7 fusion.32
  83.4 22.2 %reduce-scatter.2.cloned.1.call-done = f32[16,27,128]{2,1,0:T(8,128)} async-done(((f32[128,27,128]{2,1,0:T(8,128)}), f32[16,27,128]{2,1,0:T(8,128)}) %reduce-scatter.2.cloned.1.call-update) | async-done | bytes 221200 | tf_op jit(solution)/shard_map/reduce_scatter | solution.py:87
  105.6 1.8 copy.13
  107.4 3.7 %fusion.65 = (bf16[8,16,16,128]{3,2,1,0:T(8,128)(2,1)}, bf16[8,16,16,128]{3,2,1,0:T(8,128)(2,1)}, bf16[8,16,16,128]{3,2,1,0:T(8,128)(2,1)}, bf16[8,16,16,128]{3,...) fusion(bf16[10,18,17,128]{3,2,1,0:T(8,128)(2,1)S(1)} %get-tuple, ...), kind=kLoop, calls=%fused_computation.177 | loop fusion | bytes 18874368 | tf_op jit(solution)/shard_map/slice | solution.py:29
  111.1 32.5 %all-reduce.4.cloned.1.call-done = f32[16,27,128]{2,0,1:T(8,128)} async-done(((f32[16,27,128]{2,0,1:T(8,128)}), f32[16,27,128]{2,0,1:T(8,128)}) %all-reduce.4.cloned.1.call-update) | async-done | bytes 221200 | tf_op jit(solution)/shard_map/psum | solution.py:86
  143.6 1.1 multiply_reduce_fusion
  144.8 14.4 %all-reduce = (f32[128]{0:T(128)S(1)}, f32[128]{0:T(128)S(1)}, f32[128]{0:T(128)S(1)}) all-reduce(f32[128]{0:T(128)S(1)} %get-tuple-element.5, f32[128]{0:T(128)S(1)} %get-tuple-element.6, f32[128]{0:T(128)S(1)} %get-tuple-element.4), channel_id=1, replica_groups=mesh['gx'=2,'gy'=4,'gz'=4] {'gx','gy'}, use_global_device_ids=true, to_apply=%region_9.0 | all-reduce | flops 384 | bytes 3072 | tf_op jit(solution)/shard_map/psum | solution.py:91
  160.5 1.8 multiply_multiply_fusion
  162.3 27.9 %all_gather.3 = bf16[128,27,128]{2,0,1:T(8,128)(2,1)S(1)} all-gather(bf16[16,27,128]{2,0,1:T(8,128)(2,1)S(1)} %get-tuple-element.53), channel_id=1, replica_groups=mesh['gx'=2,'gy'=4,'gz'=4] {'gx','gy'}, dimensions={0}, use_global_device_ids=true | all-gather | bytes 995328 | tf_op jit(solution)/shard_map/all_gather | solution.py:83
  207.7 1.1 fusion.2
  (105 shorter events, 24.2 us)
Async XLA Ops:
  7.2 23.5 %copy-start = (bf16[8,16,16,128]{3,2,1,0:T(8,128)(2,1)S(1)}, bf16[8,16,16,128]{3,2,1,0:T(8,128)(2,1)}, u32[]{:S(2)}) copy-start(bf16[8,16,16,128]{3,2,1,0:T(8,128)(2,1)} %param.4) | copy-start | bytes 1572868
  7.2 98.4 %reduce-scatter.2.cloned.1.call-start = ((), (), s32[]{:S(2)}) async-start(), calls=%async_computation.1 | async-start | bytes 2359296 | tf_op jit(solution)/shard_map/reduce_scatter | solution.py:87
  8.2 3.7 %collective-permute-start = (bf16[1,16,16,128]{3,2,1,0:T(8,128)(2,1)S(1)}, bf16[1,16,16,128]{3,2,1,0:T(8,128)(2,1)S(1)}, u32[]{:S(2)}, u32[]{:S(2)}) collective-permute-start(bf16[1,16,16,128]{3,2,1,0:T(8,128)(2,1)S(1)} %get-tuple-element.51), channel_id=1, source_target_pairs={{0,16},{1,17},{2,18},{3,19},{4,20},{5,21},{6,22},{7,23},{8,24},{9,... | collective-permute-start | bytes 196616 | tf_op jit(solution)/shard_map/ppermute | solution.py:19
  10.6 3.1 %collective-permute-start.1 = (bf16[1,16,16,128]{3,2,1,0:T(8,128)(2,1)S(1)}, bf16[1,16,16,128]{3,2,1,0:T(8,128)(2,1)S(1)}, u32[]{:S(2)}, u32[]{:S(2)}) collective-permute-start(bf16[1,16,16,128]{3,2,1,0:T(8,128)(2,1)S(1)} %get-tuple-element.50), channel_id=1, source_target_pairs={{16,0},{17,1},{18,2},{19,3},{20,4},{21,5},{22,6},{23,7},{24,8},{25... | collective-permute-start | bytes 196616 | tf_op jit(solution)/shard_map/ppermute | solution.py:21
  13.3 38.8 %copy-start.29 = (bf16[9,16,16,128]{3,2,1,0:T(8,128)(2,1)}, bf16[9,16,16,128]{3,2,1,0:T(8,128)(2,1)S(1)}, u32[]{:S(2)}) copy-start(bf16[9,16,16,128]{3,2,1,0:T(8,128)(2,1)S(1)} %get-tuple-element.47) | copy-start | bytes 1769476
  13.7 20.8 %copy-start.28 = (bf16[9,16,16,128]{3,2,1,0:T(8,128)(2,1)}, bf16[9,16,16,128]{3,2,1,0:T(8,128)(2,1)S(1)}, u32[]{:S(2)}) copy-start(bf16[9,16,16,128]{3,2,1,0:T(8,128)(2,1)S(1)} %get-tuple-element.56) | copy-start | bytes 1769476
  13.8 6.6 %collective-permute-start.3 = (bf16[10,1,16,128]{3,2,1,0:T(8,128)(2,1)S(1)}, bf16[10,1,16,128]{3,2,1,0:T(8,128)(2,1)S(1)}, u32[]{:S(2)}, u32[]{:S(2)}) collective-permute-start(bf16[10,1,16,128]{3,2,1,0:T(8,128)(2,1)S(1)} %get-tuple-element.46), channel_id=1, source_target_pairs={{4,0},{8,4},{12,8},{5,1},{9,5},{13,9},{6,2},{10,6},{14,10},{7,3},{... | collective-permute-start | bytes 122888 | tf_op jit(solution)/shard_map/ppermute | solution.py:21
  15.1 6.6 %collective-permute-start.2 = (bf16[10,1,16,128]{3,2,1,0:T(8,128)(2,1)S(1)}, bf16[10,1,16,128]{3,2,1,0:T(8,128)(2,1)S(1)}, u32[]{:S(2)}, u32[]{:S(2)}) collective-permute-start(bf16[10,1,16,128]{3,2,1,0:T(8,128)(2,1)S(1)} %get-tuple-element.45), channel_id=1, source_target_pairs={{0,4},{4,8},{8,12},{1,5},{5,9},{9,13},{2,6},{6,10},{10,14},{3,7},{... | collective-permute-start | bytes 122888 | tf_op jit(solution)/shard_map/ppermute | solution.py:19
  21.8 6.5 %collective-permute-start.4 = (bf16[10,18,1,128]{3,2,1,0:T(2,128)(2,1)S(1)}, bf16[10,18,1,128]{3,2,1,0:T(2,128)(2,1)S(1)}, u32[]{:S(2)}, u32[]{:S(2)}) collective-permute-start(bf16[10,18,1,128]{3,2,1,0:T(2,128)(2,1)S(1)} %get-tuple-element.34), channel_id=1, source_target_pairs={{1,0},{2,1},{3,2},{5,4},{6,5},{7,6},{9,8},{10,9},{11,10},{13,12},{... | collective-permute-start | bytes 138248 | tf_op jit(solution)/shard_map/ppermute | solution.py:21
  23.1 6.7 %collective-permute-start.5 = (bf16[10,18,1,128]{3,2,1,0:T(2,128)(2,1)S(1)}, bf16[10,18,1,128]{3,2,1,0:T(2,128)(2,1)S(1)}, u32[]{:S(2)}, u32[]{:S(2)}) collective-permute-start(bf16[10,18,1,128]{3,2,1,0:T(2,128)(2,1)S(1)} %get-tuple-element.35), channel_id=1, source_target_pairs={{0,1},{1,2},{2,3},{4,5},{5,6},{6,7},{8,9},{9,10},{10,11},{12,13},{... | collective-permute-start | bytes 138248 | tf_op jit(solution)/shard_map/ppermute | solution.py:19
  42.3 1.0 copy-start.1
  60.2 83.5 %all-reduce.4.cloned.1.call-start = ((), (), s32[]{:S(2)}) async-start(), calls=%async_computation.2 | async-start | bytes 442368 | tf_op jit(solution)/shard_map/psum | solution.py:86
  144.8 45.7 %copy-start.22 = (bf16[8,16,16,128]{3,2,1,0:T(8,128)(2,1)S(1)}, bf16[8,16,16,128]{3,2,1,0:T(8,128)(2,1)}, u32[]{:S(2)}) copy-start(bf16[8,16,16,128]{3,2,1,0:T(8,128)(2,1)} %get-tuple-element.43) | copy-start | bytes 1572868
  190.1 1.0 copy-start.20
  190.4 1.1 copy-start.19
  191.5 1.1 copy-start.18
  191.8 1.1 copy-start.3
  192.9 1.0 copy-start.17
  193.2 1.1 copy-start.27
  194.2 1.1 copy-start.16
  194.6 1.1 copy-start.15
  195.6 1.1 copy-start.26
  196.0 1.1 copy-start.14
  197.0 1.1 copy-start.13
  197.4 1.1 copy-start.2
  198.3 1.1 copy-start.12
  198.7 1.1 copy-start.11
  199.7 1.1 copy-start.25
  200.1 1.1 copy-start.10
  201.1 1.1 copy-start.9
  201.5 1.1 copy-start.24
  202.4 1.1 copy-start.8
  202.9 1.1 copy-start.7
  203.8 1.1 copy-start.21
  204.3 1.1 copy-start.6
  205.2 1.1 copy-start.5
  205.6 1.1 copy-start.23
  206.6 1.1 copy-start.4
Sparse Core Ops, SparseCore 0:
  60.3 45.2 reduce-scatter.1
  108.5 35.0 all-reduce.3
where the time goes:
time: 217 us; the launch traced here: 216 us
  waiting for transfers between devices  59 us (27%)
  blocking collectives  58.9 us (27%)
  matrix products  35 us (16%)
  local copies, waits for them, and re-layouts  24.4 us (11%)
  starting transfers between devices  15.8 us (7%)
  between operations  15.2 us (7%)
  other arithmetic  7.2 us (3%)
    psum x1, waiting for transfers between devices, on_device(): column_sum = lax.psum(local_terms, 'gz')  32.5 us
    all_gather x1, blocking collectives, on_device(): lax.all_gather(std_float.astype(jnp.bfloat16), ('gx', 'gy'), axis=0, tile...  27.9 us
    dot_general x27, matrix products, filter_terms(): lax.dot_general(flat_in, view, (((0,), (0,)), ((), ())), preferred_elemen...  26.3 us
    reduce_scatter x1, waiting for transfers between devices, on_device(): lax.psum_scatter(column_sum, ('gx', 'gy'), scatter_dimension=0, tiled=True)  22.2 us
    psum x1, blocking collectives, on_device(): lax.psum((jnp.sum(raw_weight, axis=(0, 1)), jnp.sum(raw_weight * raw_weig...  16.7 us
    psum x1, blocking collectives, on_device(): lax.psum((local_grad, local_cross, local_square), ('gx', 'gy'))  14.4 us
    ppermute x3, starting transfers between devices, with_halo(): lax.ppermute(tail, axis, [(i, (i + 1) % count) for i in range(ends)])  11.8 us
    unnamed x61, local copies, waits for them, and re-layouts  9.64 us
  transfers between devices with their start and end apart: 8, of which 7 were waited for; matrix products, arithmetic and copies ran while one was open for 5% of the time, Pallas kernels for 0%

commit v1 on v0

--- a/solution.py
+++ b/solution.py
@@ -83,7 +83,10 @@
     std_whole = lax.all_gather(std_float.astype(jnp.bfloat16), ("gx", "gy"), axis=0, tiled=True)
     input_grad = input_rows(padded, extent, std_whole)
     local_terms = filter_terms(padded, flat_in, extent)
-    column_sum = lax.psum(local_terms, "gz")
+    size, column_sum = (lax.axis_size("gz"), local_terms)
+    for stride in [1 << k for k in range(size.bit_length() - 1)]:
+        route = [(i_2, i_2 ^ stride) for i_2 in range(size)]
+        column_sum = column_sum + lax.ppermute(column_sum, "gz", route)
     filter_grad = lax.psum_scatter(column_sum, ("gx", "gy"), scatter_dimension=0, tiled=True)
     local_grad = jnp.sum(filter_grad, axis=(0, 1))
     local_cross = jnp.sum(filter_grad * std_float, axis=(0, 1))

time: 217 us -> 280 us (1.29)
  waiting for transfers between devices: 59 us -> 133 us
  matrix products: 35 us -> 18.1 us
  starting transfers between devices: 15.8 us -> 21.2 us
  other arithmetic: 7.2 us -> 10.1 us
    ppermute x0 -> x2, waiting for transfers between devices: none -> 112 us  [on_device(): column_sum = column_sum + lax.ppermute(column_sum, 'gz', route)]
    psum x1 -> x0, waiting for transfers between devices: 32.5 us -> none  [on_device(): column_sum = lax.psum(local_terms, 'gz')]
    dot_general x27, matrix products: 26.3 us -> 9.36 us  [filter_terms(): lax.dot_general(flat_in, view, (((0,), (0,)), ((), ())), preferred_elemen...]
    ppermute x0 -> x2, starting transfers between devices: none -> 5.44 us  [on_device(): column_sum = column_sum + lax.ppermute(column_sum, 'gz', route)]
    reduce_scatter x1, waiting for transfers between devices: 22.2 us -> 17.5 us  [on_device(): lax.psum_scatter(column_sum, ('gx', 'gy'), scatter_dimension=0, tiled=True)]
    another operation x1 -> x0, local copies, waits for them, and re-layouts: 3.15 us -> none  [filter_terms(): return jnp.stack(pieces, axis=1)]
    add x0 -> x1, local copies, waits for them, and re-layouts: none -> 3.09 us  [on_device(): column_sum = column_sum + lax.ppermute(column_sum, 'gz', route)]
  transfers between devices with their start and end apart: 8 -> 9, of which waited for: 7 -> 8; matrix products, arithmetic and copies ran while one was open for 5% -> 4% of each run, Pallas kernels for 0% -> 0%
where the time goes in v1:
time: 280 us; the launch traced here: 279 us
  waiting for transfers between devices  133 us (48%)
  blocking collectives  57.7 us (21%)
  local copies, waits for them, and re-layouts  23.2 us (8%)
  starting transfers between devices  21.2 us (8%)
  matrix products  18.1 us (6%)
  between operations  15.4 us (6%)
  other arithmetic  10.1 us (4%)
    ppermute x2, waiting for transfers between devices, on_device(): column_sum = column_sum + lax.ppermute(column_sum, 'gz', route)  112 us
    all_gather x1, blocking collectives, on_device(): lax.all_gather(std_float.astype(jnp.bfloat16), ('gx', 'gy'), axis=0, tile...  27.8 us
    reduce_scatter x1, waiting for transfers between devices, on_device(): lax.psum_scatter(column_sum, ('gx', 'gy'), scatter_dimension=0, tiled=True)  17.5 us
    psum x1, blocking collectives, on_device(): lax.psum((jnp.sum(raw_weight, axis=(0, 1)), jnp.sum(raw_weight * raw_weig...  15.5 us
    psum x1, blocking collectives, on_device(): lax.psum((local_grad, local_cross, local_square), ('gx', 'gy'))  14.4 us
    ppermute x3, starting transfers between devices, with_halo(): lax.ppermute(tail, axis, [(i, (i + 1) % count) for i in range(ends)])  11.8 us
    unnamed x61, local copies, waits for them, and re-layouts  10.2 us
    dot_general x27, matrix products, filter_terms(): lax.dot_general(flat_in, view, (((0,), (0,)), ((), ())), preferred_elemen...  9.36 us
  transfers between devices with their start and end apart: 9, of which 8 were waited for; matrix products, arithmetic and copies ran while one was open for 4% of the time, Pallas kernels for 0%

profile of v1, /device:TPU:0, one launch (start us, length us, event | category | flops | bytes accessed | tf_op | source)
XLA Modules:
  0.0 279.0 jit_solution(276892713439819950)
XLA Ops:
  7.2 0.9 fusion.68
  8.2 2.4 collective-permute-start
  10.6 1.3 collective-permute-start.1
  11.9 1.4 constant_dynamic-update-slice_fusion.5
  13.3 0.4 collective-permute-done.1
  13.8 1.3 collective-permute-start.3
  15.1 4.8 %collective-permute-start.2 = (bf16[10,1,16,128]{3,2,1,0:T(8,128)(2,1)S(1)}, bf16[10,1,16,128]{3,2,1,0:T(8,128)(2,1)S(1)}, u32[]{:S(2)}, u32[]{:S(2)}) collective-permute-start(bf16[10,1,16,128]{3,2,1,0:T(8,128)(2,1)S(1)} %get-tuple-element.44), channel_id=1, source_target_pairs={{0,4},{4,8},{8,12},{1,5},{5,9},{9,13},{2,6},{6,10},{10,14},{3,7},{... | collective-permute-start | bytes 122888 | tf_op jit(solution)/shard_map/ppermute | solution.py:19
  19.9 0.4 collective-permute-done.3
  20.3 1.3 collective-permute-done.2
  21.8 1.3 collective-permute-start.4
  23.1 4.6 %collective-permute-start.5 = (bf16[10,18,1,128]{3,2,1,0:T(2,128)(2,1)S(1)}, bf16[10,18,1,128]{3,2,1,0:T(2,128)(2,1)S(1)}, u32[]{:S(2)}, u32[]{:S(2)}) collective-permute-start(bf16[10,18,1,128]{3,2,1,0:T(2,128)(2,1)S(1)} %get-tuple-element.34), channel_id=1, source_target_pairs={{0,1},{1,2},{2,3},{4,5},{5,6},{6,7},{8,9},{9,10},{10,11},{12,13},{... | collective-permute-start | bytes 138248 | tf_op jit(solution)/shard_map/ppermute | solution.py:19
  27.7 0.6 collective-permute-done.4
  28.3 1.5 collective-permute-done.5
  29.8 0.8 pad_maximum_fusion.2
  35.2 0.7 copy-done.1
  40.9 2.5 collective-permute-start.6
  43.3 37.2 %collective-permute-done.6 = f32[128,27,128]{0,2,1:T(8,128)S(1)} collective-permute-done((f32[128,27,128]{0,2,1:T(8,128)S(1)}, f32[128,27,128]{0,2,1:T(8,128)S(1)}, u32[]{:S(2)}, u32[]{:S(2)}) %collective-permute-start.6) | collective-permute-done | bytes 1769504 | tf_op jit(solution)/shard_map/ppermute | solution.py:89
  80.8 3.0 %collective-permute-start.7 = (f32[128,27,128]{0,2,1:T(8,128)S(1)}, f32[128,27,128]{0,2,1:T(8,128)S(1)}, u32[]{:S(2)}, u32[]{:S(2)}) collective-permute-start(f32[128,27,128]{0,2,1:T(8,128)S(1)} %add.136), channel_id=1, source_target_pairs={{0,2},{1,3},{2,0},{3,1},{4,6},{5,7},{6,4},{7,5},{8,10},{9,11},{10,... | collective-permute-start | bytes 5308424 | tf_op jit(solution)/shard_map/ppermute | solution.py:89
  83.8 74.3 %collective-permute-done.7 = f32[128,27,128]{0,2,1:T(8,128)S(1)} collective-permute-done((f32[128,27,128]{0,2,1:T(8,128)S(1)}, f32[128,27,128]{0,2,1:T(8,128)S(1)}, u32[]{:S(2)}, u32[]{:S(2)}) %collective-permute-start.7) | collective-permute-done | bytes 1769504 | tf_op jit(solution)/shard_map/ppermute | solution.py:89
  158.1 1.4 add.137
  159.5 3.1 %copy.12 = f32[128,27,128]{2,1,0:T(8,128)} copy(f32[128,27,128]{0,2,1:T(8,128)} %add.137) | data formatting | bytes 3538944 | tf_op jit(solution)/shard_map/add | solution.py:89
  162.6 1.0 multiply_reduce_fusion.2
  163.7 15.5 %all-reduce.1 = (f32[128]{0:T(128)S(1)}, f32[128]{0:T(128)S(1)}) all-reduce(f32[128]{0:T(128)S(1)} %get-tuple-element.7, f32[128]{0:T(128)S(1)} %get-tuple-element.6), channel_id=1, replica_groups=mesh['gx'=2,'gy'=4,'gz'=4] {'gx','gy'}, use_global_device_ids=true, to_apply=%region_1.0 | all-reduce | flops 256 | bytes 2048 | tf_op jit(solution)/shard_map/psum | solution.py:75
  179.2 1.9 slice.299
  181.1 1.9 slice.338
  183.0 1.8 fusion.32
  184.7 3.7 %fusion.65 = (bf16[8,16,16,128]{3,2,1,0:T(8,128)(2,1)}, bf16[8,16,16,128]{3,2,1,0:T(8,128)(2,1)}, bf16[8,16,16,128]{3,2,1,0:T(8,128)(2,1)}, bf16[8,16,16,128]{3,...) fusion(bf16[10,18,17,128]{3,2,1,0:T(8,128)(2,1)S(1)} %get-tuple, ...), kind=kLoop, calls=%fused_computation.177 | loop fusion | bytes 18874368 | tf_op jit(solution)/shard_map/slice | solution.py:29
  188.5 17.5 %reduce-scatter.2.cloned.1.call-done = f32[16,27,128]{2,1,0:T(8,128)} async-done(((f32[128,27,128]{2,1,0:T(8,128)}), f32[16,27,128]{2,1,0:T(8,128)}) %reduce-scatter.2.cloned.1.call-update) | async-done | bytes 221200 | tf_op jit(solution)/shard_map/reduce_scatter | solution.py:90
  205.9 1.0 multiply_reduce_fusion
  206.9 1.2 multiply_reduce_fusion.1
  208.1 14.4 %all-reduce = (f32[128]{0:T(128)S(1)}, f32[128]{0:T(128)S(1)}, f32[128]{0:T(128)S(1)}) all-reduce(f32[128]{0:T(128)S(1)} %multiply_reduce_fusion.1, f32[128]{0:T(128)S(1)} %get-tuple-element.5, f32[128]{0:T(128)S(1)} %get-tuple-element.4), channel_id=1, replica_groups=mesh['gx'=2,'gy'=4,'gz'=4] {'gx','gy'}, use_global_device_ids=true, to_apply=%region_8.0 | all-reduce | flops 384 | bytes 3072 | tf_op jit(solution)/shard_map/psum | solution.py:94
  222.5 0.6 broadcast_multiply_fusion.1
  223.8 1.9 multiply_multiply_fusion
  225.7 27.8 %all_gather.3 = bf16[128,27,128]{2,0,1:T(8,128)(2,1)S(1)} all-gather(bf16[16,27,128]{2,0,1:T(8,128)(2,1)S(1)} %get-tuple-element.52), channel_id=1, replica_groups=mesh['gx'=2,'gy'=4,'gz'=4] {'gx','gy'}, dimensions={0}, use_global_device_ids=true | all-gather | bytes 995328 | tf_op jit(solution)/shard_map/all_gather | solution.py:83
  254.1 0.4 copy-done.20
  255.2 0.7 copy-done.18
  256.6 0.7 copy-done.17
  258.0 0.7 copy-done.16
  259.3 0.7 copy-done.26
  260.7 0.7 copy-done.13
  262.1 0.6 copy-done.12
  263.5 0.6 copy-done.25
  264.9 0.6 copy-done.9
  266.2 0.6 copy-done.8
  267.6 0.6 copy-done.21
  269.0 0.6 copy-done.5
  270.4 0.6 copy-done.4
  271.0 1.1 fusion.2
  (108 shorter events, 18.7 us)
Async XLA Ops:
  7.2 23.5 %copy-start = (bf16[8,16,16,128]{3,2,1,0:T(8,128)(2,1)S(1)}, bf16[8,16,16,128]{3,2,1,0:T(8,128)(2,1)}, u32[]{:S(2)}) copy-start(bf16[8,16,16,128]{3,2,1,0:T(8,128)(2,1)} %param.4) | copy-start | bytes 1572868
  7.2 198.7 %reduce-scatter.2.cloned.1.call-start = ((), (), s32[]{:S(2)}) async-start(), calls=%async_computation.1 | async-start | bytes 2359296 | tf_op jit(solution)/shard_map/reduce_scatter | solution.py:90
  8.2 3.7 %collective-permute-start = (bf16[1,16,16,128]{3,2,1,0:T(8,128)(2,1)S(1)}, bf16[1,16,16,128]{3,2,1,0:T(8,128)(2,1)S(1)}, u32[]{:S(2)}, u32[]{:S(2)}) collective-permute-start(bf16[1,16,16,128]{3,2,1,0:T(8,128)(2,1)S(1)} %get-tuple-element.50), channel_id=1, source_target_pairs={{0,16},{1,17},{2,18},{3,19},{4,20},{5,21},{6,22},{7,23},{8,24},{9,... | collective-permute-start | bytes 196616 | tf_op jit(solution)/shard_map/ppermute | solution.py:19
  10.6 3.1 %collective-permute-start.1 = (bf16[1,16,16,128]{3,2,1,0:T(8,128)(2,1)S(1)}, bf16[1,16,16,128]{3,2,1,0:T(8,128)(2,1)S(1)}, u32[]{:S(2)}, u32[]{:S(2)}) collective-permute-start(bf16[1,16,16,128]{3,2,1,0:T(8,128)(2,1)S(1)} %get-tuple-element.49), channel_id=1, source_target_pairs={{16,0},{17,1},{18,2},{19,3},{20,4},{21,5},{22,6},{23,7},{24,8},{25... | collective-permute-start | bytes 196616 | tf_op jit(solution)/shard_map/ppermute | solution.py:21
  13.3 25.8 %copy-start.29 = (bf16[9,16,16,128]{3,2,1,0:T(8,128)(2,1)}, bf16[9,16,16,128]{3,2,1,0:T(8,128)(2,1)S(1)}, u32[]{:S(2)}) copy-start(bf16[9,16,16,128]{3,2,1,0:T(8,128)(2,1)S(1)} %get-tuple-element.46) | copy-start | bytes 1769476
  13.7 18.3 %copy-start.28 = (bf16[9,16,16,128]{3,2,1,0:T(8,128)(2,1)}, bf16[9,16,16,128]{3,2,1,0:T(8,128)(2,1)S(1)}, u32[]{:S(2)}) copy-start(bf16[9,16,16,128]{3,2,1,0:T(8,128)(2,1)S(1)} %get-tuple-element.55) | copy-start | bytes 1769476
  13.8 6.6 %collective-permute-start.3 = (bf16[10,1,16,128]{3,2,1,0:T(8,128)(2,1)S(1)}, bf16[10,1,16,128]{3,2,1,0:T(8,128)(2,1)S(1)}, u32[]{:S(2)}, u32[]{:S(2)}) collective-permute-start(bf16[10,1,16,128]{3,2,1,0:T(8,128)(2,1)S(1)} %get-tuple-element.45), channel_id=1, source_target_pairs={{4,0},{8,4},{12,8},{5,1},{9,5},{13,9},{6,2},{10,6},{14,10},{7,3},{... | collective-permute-start | bytes 122888 | tf_op jit(solution)/shard_map/ppermute | solution.py:21
  15.1 6.6 %collective-permute-start.2 = (bf16[10,1,16,128]{3,2,1,0:T(8,128)(2,1)S(1)}, bf16[10,1,16,128]{3,2,1,0:T(8,128)(2,1)S(1)}, u32[]{:S(2)}, u32[]{:S(2)}) collective-permute-start(bf16[10,1,16,128]{3,2,1,0:T(8,128)(2,1)S(1)} %get-tuple-element.44), channel_id=1, source_target_pairs={{0,4},{4,8},{8,12},{1,5},{5,9},{9,13},{2,6},{6,10},{10,14},{3,7},{... | collective-permute-start | bytes 122888 | tf_op jit(solution)/shard_map/ppermute | solution.py:19
  21.8 6.5 %collective-permute-start.4 = (bf16[10,18,1,128]{3,2,1,0:T(2,128)(2,1)S(1)}, bf16[10,18,1,128]{3,2,1,0:T(2,128)(2,1)S(1)}, u32[]{:S(2)}, u32[]{:S(2)}) collective-permute-start(bf16[10,18,1,128]{3,2,1,0:T(2,128)(2,1)S(1)} %get-tuple-element.33), channel_id=1, source_target_pairs={{1,0},{2,1},{3,2},{5,4},{6,5},{7,6},{9,8},{10,9},{11,10},{13,12},{... | collective-permute-start | bytes 138248 | tf_op jit(solution)/shard_map/ppermute | solution.py:21
  23.1 6.7 %collective-permute-start.5 = (bf16[10,18,1,128]{3,2,1,0:T(2,128)(2,1)S(1)}, bf16[10,18,1,128]{3,2,1,0:T(2,128)(2,1)S(1)}, u32[]{:S(2)}, u32[]{:S(2)}) collective-permute-start(bf16[10,18,1,128]{3,2,1,0:T(2,128)(2,1)S(1)} %get-tuple-element.34), channel_id=1, source_target_pairs={{0,1},{1,2},{2,3},{4,5},{5,6},{6,7},{8,9},{9,10},{10,11},{12,13},{... | collective-permute-start | bytes 138248 | tf_op jit(solution)/shard_map/ppermute | solution.py:19
  34.9 1.0 copy-start.1
  40.9 39.7 %collective-permute-start.6 = (f32[128,27,128]{0,2,1:T(8,128)S(1)}, f32[128,27,128]{0,2,1:T(8,128)S(1)}, u32[]{:S(2)}, u32[]{:S(2)}) collective-permute-start(f32[128,27,128]{0,2,1:T(8,128)S(1)} %fusion.11), channel_id=1, source_target_pairs={{0,1},{1,0},{2,3},{3,2},{4,5},{5,4},{6,7},{7,6},{8,9},{9,8},{10,11... | collective-permute-start | bytes 5308424 | tf_op jit(solution)/shard_map/ppermute | solution.py:89
  80.8 77.3 %collective-permute-start.7 = (f32[128,27,128]{0,2,1:T(8,128)S(1)}, f32[128,27,128]{0,2,1:T(8,128)S(1)}, u32[]{:S(2)}, u32[]{:S(2)}) collective-permute-start(f32[128,27,128]{0,2,1:T(8,128)S(1)} %add.136), channel_id=1, source_target_pairs={{0,2},{1,3},{2,0},{3,1},{4,6},{5,7},{6,4},{7,5},{8,10},{9,11},{10,... | collective-permute-start | bytes 5308424 | tf_op jit(solution)/shard_map/ppermute | solution.py:89
  208.1 45.7 %copy-start.22 = (bf16[8,16,16,128]{3,2,1,0:T(8,128)(2,1)S(1)}, bf16[8,16,16,128]{3,2,1,0:T(8,128)(2,1)}, u32[]{:S(2)}) copy-start(bf16[8,16,16,128]{3,2,1,0:T(8,128)(2,1)} %get-tuple-element.42) | copy-start | bytes 1572868
  253.5 1.0 copy-start.20
  253.8 1.1 copy-start.19
  254.8 1.1 copy-start.18
  255.2 1.1 copy-start.3
  256.3 1.0 copy-start.17
  256.6 1.1 copy-start.27
  257.6 1.1 copy-start.16
  258.0 1.1 copy-start.15
  259.0 1.1 copy-start.26
  259.3 1.1 copy-start.14
  260.3 1.1 copy-start.13
  260.7 1.1 copy-start.2
  261.7 1.1 copy-start.12
  262.1 1.1 copy-start.11
  263.1 1.1 copy-start.25
  263.5 1.1 copy-start.10
  264.4 1.1 copy-start.9
  264.9 1.1 copy-start.24
  265.8 1.1 copy-start.8
  266.2 1.1 copy-start.7
  267.2 1.1 copy-start.21
  267.6 1.1 copy-start.6
  268.6 1.1 copy-start.5
  269.0 1.1 copy-start.23
  269.9 1.1 copy-start.4
Sparse Core Ops, SparseCore 0:
  162.8 43.0 reduce-scatter.1
